TPU v7x, 32 devices: a whole 2x2x4 slice. The times are simulated.
32 devices in a mesh: rep: 4 (over z), data: 8 (over y, x, core).
Axes of the slice: x: 2, y: 2, z: 4, core: 2. Of those that a mesh axis runs over, the one named last changes fastest.
Arguments:
- x_in: bfloat16 [256, 32, 512], P(('rep', 'data'))
- d_out: float32 [256, 32, 512], P(('rep', 'data'))
- weights: bfloat16 [6, 1024, 2048], replicated
- biases: float32 [6, 2048], replicated
Outputs:
- output 1: float32 [6, 1024, 2048], replicated
- output 2: float32 [6, 2048], replicated
- output 3: float32 [256, 32, 512], P(('rep', 'data'))
All inputs are finite; a program needn't handle non-finite values.
Results may differ from a plain program's by a relative error of at most 0.00449199.
Values are sent between devices in bfloat16 or wider.
A program may use at most 1 GiB of HBM per device.

v0:
```python
import functools

import jax
import jax.numpy as jnp
from jax import lax
from jax.experimental import pallas as pl
from jax.experimental.pallas import tpu as pltpu
from jax.sharding import PartitionSpec as P

MESH = pl.DeviceIdType.MESH
H = 512
G = 4 * H
T = 4
HB = 256


def sigmoid(z):
    return 0.5 * jnp.tanh(0.5 * z) + 0.5


def stack_kernel(steps, half, layers, x_ref, dy_ref, w_hbm, b_ref, dw_hbm, db_ref, dx_ref,
                 w, wt, xs, hs, gates, cs, xp, dzs, dys, xb, dyb, dxs, dr_s, dc_s, dbacc, xt, stage,
                 w_sem, in_send, in_recv, fsend, frecv, bsend, brecv, dx_send, dx_recv, out_sem):
    rows = 2 * half
    chunk = T * rows
    n_chunks = steps // T
    me = lax.axis_index("data")
    core = lax.rem(me, 2)
    partner = me + 1 - 2 * core
    first = core * layers

    barrier = pltpu.get_barrier_semaphore()
    pl.semaphore_signal(barrier, inc=1, device_id={"data": partner}, device_id_type=MESH)

    def weight_copy(l):
        return pltpu.make_async_copy(w_hbm.at[first + l], w.at[l], w_sem.at[l])

    for l in range(layers):
        weight_copy(l).start()
    pl.semaphore_wait(barrier, 1)

    def x_copy():
        return pltpu.make_async_remote_copy(src_ref=x_ref, dst_ref=xb, send_sem=in_send.at[0], recv_sem=in_recv.at[0],
                                            device_id={"data": partner}, device_id_type=MESH)

    def dy_copy():
        return pltpu.make_async_remote_copy(src_ref=dy_ref, dst_ref=dyb, send_sem=in_send.at[1], recv_sem=in_recv.at[1],
                                            device_id={"data": partner}, device_id_type=MESH)

    def chunk_rows(k):
        return pl.ds(pl.multiple_of(k * chunk, chunk), chunk)

    def f_copy(k):
        return pltpu.make_async_remote_copy(src_ref=xs.at[layers, chunk_rows(k)], dst_ref=xs.at[0, chunk_rows(k)],
                                            send_sem=fsend.at[k], recv_sem=frecv.at[k],
                                            device_id={"data": partner}, device_id_type=MESH)

    def b_copy(k):
        return pltpu.make_async_remote_copy(src_ref=dys.at[1, chunk_rows(k)], dst_ref=dys.at[0, chunk_rows(k)],
                                            send_sem=bsend.at[k], recv_sem=brecv.at[k],
                                            device_id={"data": partner}, device_id_type=MESH)

    def dx_copy():
        return pltpu.make_async_remote_copy(src_ref=dxs, dst_ref=dx_ref, send_sem=dx_send, recv_sem=dx_recv,
                                            device_id={"data": partner}, device_id_type=MESH)

    @pl.when(core == 1)
    def _():
        x_copy().start()

    @pl.when(core == 0)
    def _():
        dy_copy().start()

    for l in range(layers):
        hs[l, :rows, :] = jnp.zeros((rows, H), jnp.bfloat16)
        cs[l, :rows, :] = jnp.zeros((rows, H), jnp.float32)
    dr_s[...] = jnp.zeros_like(dr_s)
    dc_s[...] = jnp.zeros_like(dc_s)
    dbacc[...] = jnp.zeros_like(dbacc)

    @pl.when(core == 0)
    def _():
        x_copy().wait_recv()

        def join(t, carry):
            both = jnp.concatenate([x_ref[t].astype(jnp.float32), xb[t].astype(jnp.float32)], axis=0)
            xs[0, pl.ds(pl.multiple_of(t * rows, rows), rows), :] = both.astype(jnp.bfloat16)
            return carry

        lax.fori_loop(0, steps, join, 0)

    def fwd_layer(k, l):
        @pl.when(k == 0)
        def _():
            weight_copy(l).wait()

        bias = b_ref[pl.ds(first + l, 1), :]
        x_chunk = xs[l, chunk_rows(k), :]
        for q in range(4):
            cols = slice(q * H, (q + 1) * H)
            xp[:, cols] = jnp.dot(x_chunk, w[l, :H, cols], preferred_element_type=jnp.float32) + bias[:, cols]

        def step(s, carry):
            t = k * T + s
            now = pl.ds(pl.multiple_of(t * rows, rows), rows)
            nxt = pl.ds(pl.multiple_of(t * rows + rows, rows), rows)
            loc = pl.ds(pl.multiple_of(s * rows, rows), rows)
            h_prev = hs[l, now, :]
            for j in range(H // HB):
                part = []
                for q in range(4):
                    cols = slice(q * H + j * HB, q * H + (j + 1) * HB)
                    part.append(xp[loc, cols] + jnp.dot(h_prev, w[l, H:, cols], preferred_element_type=jnp.float32))
                hc = slice(j * HB, (j + 1) * HB)
                in_g, fg_g, cand_g, out_g = sigmoid(part[0]), sigmoid(part[1]), jnp.tanh(part[2]), sigmoid(part[3])
                c_new = fg_g * cs[l, now, hc] + in_g * cand_g
                h_new = out_g * jnp.tanh(c_new)
                cs[l, nxt, hc] = c_new
                hs[l, nxt, hc] = h_new.astype(jnp.bfloat16)
                xs[l + 1, now, hc] = (h_new + xs[l, now, hc].astype(jnp.float32)).astype(jnp.bfloat16)
                for q, gate in enumerate((in_g, fg_g, cand_g, out_g)):
                    gates[l, now, q * H + j * HB:q * H + (j + 1) * HB] = gate
            return carry

        lax.fori_loop(0, T, step, 0)

    def fwd_chunk(k, carry):
        @pl.when(core == 1)
        def _():
            f_copy(k).wait_recv()

        def layer(l, c):
            fwd_layer(k, l)
            return c

        lax.fori_loop(0, layers, layer, 0)

        @pl.when(core == 0)
        def _():
            f_copy(k).start()

        return carry

    lax.fori_loop(0, n_chunks, fwd_chunk, 0)

    def transpose_weights(i, carry):
        l = i // 8
        j = lax.rem(i, 8)
        cols = pl.ds(pl.multiple_of(j * 256, 256), 256)
        wt[l, cols, :] = w[l, :, cols].T
        return carry

    lax.fori_loop(0, layers * 8, transpose_weights, 0)

    @pl.when(core == 1)
    def _():
        dy_copy().wait_recv()

        def join(t, carry):
            dys[0, pl.ds(pl.multiple_of(t * rows, rows), rows), :] = jnp.concatenate([dyb[t], dy_ref[t]], axis=0)
            return carry

        lax.fori_loop(0, steps, join, 0)

    def bwd_layer(k, l, src):
        def step(i, carry):
            t = k * T + (T - 1 - i)
            now = pl.ds(pl.multiple_of(t * rows, rows), rows)
            nxt = pl.ds(pl.multiple_of(t * rows + rows, rows), rows)
            acc = jnp.zeros((rows, H), jnp.float32)
            for j in range(H // HB):
                hc = slice(j * HB, (j + 1) * HB)
                gc = [slice(q * H + j * HB, q * H + (j + 1) * HB) for q in range(4)]
                in_g, fg_g, cand_g, out_g = (gates[l, now, c] for c in gc)
                tanh_c = jnp.tanh(cs[l, nxt, hc])
                dh = dys[src, now, hc] + dr_s[l, :, hc]
                dc = dc_s[l, :, hc] + dh * out_g * (1.0 - tanh_c * tanh_c)
                dc_s[l, :, hc] = dc * fg_g
                dz = (dc * cand_g * in_g * (1.0 - in_g), dc * cs[l, now, hc] * fg_g * (1.0 - fg_g),
                      dc * in_g * (1.0 - cand_g * cand_g), dh * tanh_c * out_g * (1.0 - out_g))
                for q in range(4):
                    low = dz[q].astype(jnp.bfloat16)
                    dbacc[l, :, gc[q]] += dz[q]
                    dzs[l, now, gc[q]] = low
                    acc += jnp.dot(low, wt[l, gc[q], H:], preferred_element_type=jnp.float32)
            dr_s[l] = acc
            return carry

        lax.fori_loop(0, T, step, 0)
        r = chunk_rows(k)
        dys[1, r, :] = dys[src, r, :] + jnp.dot(dzs[l, r, :], wt[l, :, :H], preferred_element_type=jnp.float32)

    def bwd_chunk(i, carry):
        k = n_chunks - 1 - i

        @pl.when(core == 0)
        def _():
            b_copy(k).wait_recv()

        def layer(j, c):
            l = layers - 1 - j
            bwd_layer(k, l, jnp.minimum(j, 1))
            return c

        lax.fori_loop(0, layers, layer, 0)

        @pl.when(core == 1)
        def _():
            b_copy(k).start()

        return carry

    lax.fori_loop(0, n_chunks, bwd_chunk, 0)

    @pl.when(core == 0)
    def _():
        def split(t, carry):
            both = dys[1, pl.ds(pl.multiple_of(t * rows, rows), rows), :]
            dx_ref[t] = both[:half]
            dxs[t] = both[half:]
            return carry

        lax.fori_loop(0, steps, split, 0)
        dx_copy().start()

    for l in range(layers):
        db_ref[pl.ds(l, 1), :] = jnp.sum(dbacc[l], axis=0, keepdims=True)

    n_rows = steps * rows

    def out_copy(i):
        l = i // 4
        b = lax.rem(i, 4)
        return pltpu.make_async_copy(stage.at[lax.rem(i, 2)], dw_hbm.at[l, pl.ds(pl.multiple_of(b * 256, 256), 256)],
                                     out_sem.at[lax.rem(i, 2)])

    def dw_block(i, carry):
        l = i // 4
        b = lax.rem(i, 4)

        @pl.when(i >= 2)
        def _():
            out_copy(i - 2).wait()

        cols = pl.ds(pl.multiple_of(lax.rem(b, 2) * 256, 256), 256)

        @pl.when(b < 2)
        def _():
            xt[...] = xs[l, :, cols].T

        @pl.when(b >= 2)
        def _():
            xt[...] = hs[l, :n_rows, cols].T

        for q in range(4):
            stage[lax.rem(i, 2), :, q * H:(q + 1) * H] = jnp.dot(xt[...], dzs[l, :, q * H:(q + 1) * H],
                                                                preferred_element_type=jnp.float32)
        out_copy(i).start()
        return carry

    lax.fori_loop(0, layers * 4, dw_block, 0)
    out_copy(layers * 4 - 2).wait()
    out_copy(layers * 4 - 1).wait()

    @pl.when(core == 0)
    def _():
        dy_copy().wait_send()
        dx_copy().wait_send()

        def drain(k, carry):
            f_copy(k).wait_send()
            return carry

        lax.fori_loop(0, n_chunks, drain, 0)

    @pl.when(core == 1)
    def _():
        x_copy().wait_send()
        dx_copy().wait_recv()

        def drain(k, carry):
            b_copy(k).wait_send()
            return carry

        lax.fori_loop(0, n_chunks, drain, 0)


def run_stack(x_t, dy_t, weights, biases):
    steps, half, _ = x_t.shape
    layers = weights.shape[0] // 2
    rows = 2 * half
    n = steps * rows
    n_chunks = steps // T
    vmem = pl.BlockSpec(memory_space=pltpu.VMEM)
    hbm = pl.BlockSpec(memory_space=pl.ANY)
    bf, f32 = jnp.bfloat16, jnp.float32
    dma = pltpu.SemaphoreType.DMA
    return pl.pallas_call(
        functools.partial(stack_kernel, steps, half, layers),
        out_shape=(jax.ShapeDtypeStruct((layers, 2 * H, G), f32), jax.ShapeDtypeStruct((layers, G), f32),
                   jax.ShapeDtypeStruct((steps, half, H), f32)),
        in_specs=[vmem, vmem, hbm, vmem],
        out_specs=(hbm, vmem, vmem),
        scratch_shapes=[
            pltpu.VMEM((layers, 2 * H, G), bf), pltpu.VMEM((layers, G, 2 * H), bf),
            pltpu.VMEM((layers + 1, n, H), bf), pltpu.VMEM((layers, n + rows, H), bf),
            pltpu.VMEM((layers, n, G), f32), pltpu.VMEM((layers, n + rows, H), f32),
            pltpu.VMEM((T * rows, G), f32), pltpu.VMEM((layers, n, G), bf),
            pltpu.VMEM((2, n, H), f32), pltpu.VMEM((steps, half, H), bf),
            pltpu.VMEM((steps, half, H), f32), pltpu.VMEM((steps, half, H), f32),
            pltpu.VMEM((layers, rows, H), f32), pltpu.VMEM((layers, rows, H), f32),
            pltpu.VMEM((layers, rows, G), f32), pltpu.VMEM((256, n), bf), pltpu.VMEM((2, 256, G), f32),
            dma((layers,)), dma((2,)), dma((2,)), dma((n_chunks,)), dma((n_chunks,)), dma((n_chunks,)), dma((n_chunks,)),
            dma, dma, dma((2,)),
        ],
        compiler_params=pltpu.CompilerParams(collective_id=0, has_side_effects=True, vmem_limit_bytes=66_000_000),
        name="stack",
    )(x_t, dy_t, weights, biases)


def solution(mesh):
    batch_axes = tuple(mesh.axis_names)

    def device_step(x_in, d_out, weights, biases):
        dw, db, dx = run_stack(jnp.swapaxes(x_in, 0, 1), jnp.swapaxes(d_out, 0, 1), weights, biases)
        top = lax.rem(lax.axis_index("data"), 2) == 1
        dw_all = jnp.concatenate([jnp.where(top, 0.0, dw), jnp.where(top, dw, 0.0)])
        db_all = jnp.concatenate([jnp.where(top, 0.0, db), jnp.where(top, db, 0.0)])
        return lax.psum(dw_all, batch_axes), lax.psum(db_all, batch_axes), jnp.swapaxes(dx, 0, 1)

    return jax.shard_map(device_step, mesh=mesh,
                         in_specs=(P(batch_axes), P(batch_axes), P(), P()),
                         out_specs=(P(), P(), P(batch_axes)), check_vma=False)
```

profile of v0, /device:TPU:0, one launch (start us, length us, event | category | flops | bytes accessed | tf_op | source)
XLA Modules:
  0.0 975.6 jit_solution(2987290064349408983)
XLA Ops:
  7.2 0.0 all-reduce.2.cloned.1.call-start
  7.2 2.1 copy.12
  9.4 1.8 copy.13
  11.2 137.4 %stack.1 = (f32[3,1024,2048]{2,1,0:T(8,128)}, f32[3,2048]{1,0:T(4,128)}, f32[32,8,512]{2,1,0:T(8,128)}) custom-call(bf16[32,8,512]{2,1,0:T(8,128)(2,1)} %bitcast.8, f32[32,8,512]{2,1,0:T(8,128)} %bitcast.7, bf16[6,1024,2048]{2,1,0:T(8,128)(2,1)} %w_hbm.1, f32[6,2048]{1,0:T(8,128)} %b_ref.1), custom_call_target="tpu_custom_call" | custom-call | tf_op jit(solution)/shard_map/stack/pallas_call | solution.py:299
  148.5 25.7 %broadcast_select_fusion.1 = (f32[3,1024,2048]{2,1,0:T(8,128)}, f32[3,1024,2048]{2,1,0:T(8,128)}) fusion(f32[3,1024,2048]{2,1,0:T(8,128)} %get-tuple-element.6, pred[]{:T(512)S(6)} %eq.3), kind=kLoop, calls=%fused_computation.2 | loop fusion | flops 12582912 | bytes 75497472 | tf_op jit(solution)/shard_map/jit(_where)/select_n | solution.py:328
  174.3 34.5 %pad_maximum_fusion = f32[6,1024,2048]{2,1,0:T(8,128)} fusion(f32[3,1024,2048]{2,1,0:T(8,128)} %get-tuple-element.13, f32[3,1024,2048]{2,1,0:T(8,128)} %get-tuple-element.12), kind=kLoop, calls=%fused_computation | loop fusion | flops 12582912 | bytes 100663296 | tf_op jit(solution)/shard_map/concatenate | solution.py:328
  208.8 0.0 copy-start
  208.8 0.0 copy-start.1
  208.8 0.0 all-reduce.2.cloned.1.call-update
  208.8 1.0 copy-done
  209.8 1.1 copy.9
  210.9 0.0 copy-done.1
  210.9 43.9 %psum.15 = f32[6,2048]{1,0:T(8,128)} all-reduce(f32[6,2048]{1,0:T(8,128)S(1)} %pad_maximum_fusion.1), channel_id=1, replica_groups=mesh['rep'=4,'data'=8] {'rep','data'}, use_global_device_ids=true, to_apply=%region_1.2 | all-reduce | flops 12288 | bytes 98304 | tf_op jit(solution)/shard_map/psum | solution.py:330
  254.8 679.4 %all-reduce.2.cloned.1.call-done = f32[6,1024,2048]{2,1,0:T(8,128)} async-done(((f32[6,1024,2048]{2,1,0:T(8,128)}), f32[6,1024,2048]{2,1,0:T(8,128)}) %all-reduce.2.cloned.1.call-update) | async-done | bytes 50331664 | tf_op jit(solution)/shard_map/psum | solution.py:330
  934.3 34.5 %copy.15 = f32[6,1024,2048]{2,1,0:T(8,128)} copy(f32[6,1024,2048]{2,1,0:T(8,128)} %all-reduce.2.cloned.1.call-done) | data formatting | bytes 100663296
  (2 shorter events, 0.0 us)
Async XLA Ops:
  7.2 927.1 %all-reduce.2.cloned.1.call-start = ((), (), s32[]{:S(2)}) async-start(), calls=%async_computation | async-start | bytes 100663296 | tf_op jit(solution)/shard_map/psum | solution.py:330
  208.8 1.0 copy-start
  208.8 2.1 copy-start.1
Sparse Core Ops, SparseCore 0:
  208.9 725.2 all-reduce.1
where the time goes:
time: 976 us
  waiting for transfers between devices  679 us (70%)
  Pallas kernels  137 us (14%)
  other arithmetic  60.3 us (6%)
  blocking collectives  43.9 us (4%)
  local copies, waits for them, and re-layouts  40.6 us (4%)
  between operations  14.1 us (1%)
    psum x1, waiting for transfers between devices, device_step(): lax.psum(dw_all, batch_axes)  679 us
    pallas_call x1, Pallas kernels, run_stack(): pl.pallas_call(functools.partial(stack_kernel, steps, half, layers), out_...  137 us
    psum x1, blocking collectives, device_step(): lax.psum(db_all, batch_axes)  43.9 us
    unnamed x8, local copies, waits for them, and re-layouts  40.6 us
    concatenate x1, other arithmetic, device_step(): dw_all = jnp.concatenate([jnp.where(top, 0.0, dw), jnp.where(top, dw, 0.0)])  34.5 us
    select_n x1, other arithmetic, device_step(): dw_all = jnp.concatenate([jnp.where(top, 0.0, dw), jnp.where(top, dw, 0.0)])  25.7 us
  transfers between devices with their start and end apart: 1, of which 1 were waited for; matrix products, arithmetic and copies ran while one was open for 0% of the time, Pallas kernels for 0%

commit v1 on v0

--- a/solution.py
+++ b/solution.py
@@ -224,6 +224,7 @@
         lax.fori_loop(0, steps, split, 0)
         dx_copy().start()
 
+    db_ref[...] = jnp.zeros_like(db_ref)
     for l in range(layers):
         db_ref[pl.ds(l, 1), :] = jnp.sum(dbacc[l], axis=0, keepdims=True)
 
@@ -298,7 +299,7 @@
     dma = pltpu.SemaphoreType.DMA
     return pl.pallas_call(
         functools.partial(stack_kernel, steps, half, layers),
-        out_shape=(jax.ShapeDtypeStruct((layers, 2 * H, G), f32), jax.ShapeDtypeStruct((layers, G), f32),
+        out_shape=(jax.ShapeDtypeStruct((layers, 2 * H, G), f32), jax.ShapeDtypeStruct((8, G), f32),
                    jax.ShapeDtypeStruct((steps, half, H), f32)),
         in_specs=[vmem, vmem, hbm, vmem],
         out_specs=(hbm, vmem, vmem),
@@ -319,15 +320,206 @@
     )(x_t, dy_t, weights, biases)
 
 
+BLOCKS = 4
+ORDERS = ((("x", "y", "z1", "z2"),) * BLOCKS,
+          (("y", "x", "z1", "z2"),) * BLOCKS,
+          (("z1", "x", "y", "z2"), ("z1", "y", "x", "z2")) * (BLOCKS // 2))
+
+
+def event_order(layers):
+    free = {"x": 0.0, "y": 0.0, "z": 0.0}
+    pending = []
+
+    def send(now, c, s, step, dim, size):
+        link = dim[0]
+        start = max(now, free[link])
+        free[link] = start + size * (1.5 if dim == "z2" else 1.0)
+        pending.append((free[link] + 0.1, s, c, step))
+
+    for s in range(BLOCKS):
+        for c in range(layers):
+            send(0.0, c, s, 0, ORDERS[c][s][0], 1.0)
+    order = []
+    while pending:
+        pending.sort()
+        now, s, c, step = pending.pop(0)
+        order.append((c, s, step))
+        if step < 7:
+            p = step + 1 if step < 3 else 6 - step
+            send(now, c, s, step + 1, ORDERS[c][s][p], 0.5 ** p)
+    return order
+
+
+def sum_kernel(layers, dw_in, db_in, dw_out, db_out, loc, land0, land1, land2, land3, dbl, dba,
+               loc_sem, put_sem, rs_send, rs_recv, ag_send, ag_recv, c_send, c_recv, db_send, db_recv):
+    land = (land0, land1, land2, land3)
+    z = lax.axis_index("rep")
+    d = lax.axis_index("data")
+    core = lax.rem(d, 2)
+    x_bit = lax.rem(d // 2, 2)
+    y_bit = d // 4
+    z1_bit = lax.rem(z, 2)
+    z2_bit = z // 2
+    bits = {"x": x_bit, "y": y_bit, "z1": z1_bit, "z2": z2_bit}
+    peer = {"x": (z, d + 2 - 4 * x_bit), "y": (z, d + 4 - 8 * y_bit), "z1": (z + 1 - 2 * z1_bit, d),
+            "z2": (z + 2 - 4 * z2_bit, d), "c": (z, d + 1 - 2 * core)}
+    first = core * layers
+    block = dw_in.shape[1] // BLOCKS
+
+    barrier = pltpu.get_barrier_semaphore()
+    for p in peer.values():
+        pl.semaphore_signal(barrier, inc=1, device_id=p, device_id_type=MESH)
+    pl.semaphore_wait(barrier, len(peer))
+
+    def rows(off, size):
+        return pl.ds(pl.multiple_of(off, 8), size)
+
+    def offset(c, s, steps):
+        off = s * block
+        for p in range(steps):
+            off = off + bits[ORDERS[c][s][p]] * (block >> (p + 1))
+        return off
+
+    def local_load(c, s):
+        return pltpu.make_async_copy(dw_in.at[c, rows(offset(c, s, 1), block // 2)], loc.at[c, s], loc_sem.at[c, s])
+
+    def reduce_copy(c, s, p):
+        dim = ORDERS[c][s][p]
+        size = block >> (p + 1)
+        if p == 0:
+            src = dw_in.at[c, rows(s * block + (1 - bits[dim]) * size, size)]
+        else:
+            src = land[p - 1].at[c, s, rows((1 - bits[dim]) * size, size)]
+        return pltpu.make_async_remote_copy(src_ref=src, dst_ref=land[p].at[c, s], send_sem=rs_send.at[c, s, p],
+                                            recv_sem=rs_recv.at[c, s, p], device_id=peer[dim], device_id_type=MESH)
+
+    def put(c, s):
+        return pltpu.make_async_copy(land3.at[c, s], dw_out.at[first + c, rows(offset(c, s, 4), block // 16)],
+                                     put_sem.at[c, s])
+
+    def gather_copy(c, s, p):
+        dim = ORDERS[c][s][p]
+        where = dw_out.at[first + c, rows(offset(c, s, p + 1), block >> (p + 1))]
+        return pltpu.make_async_remote_copy(src_ref=land3.at[c, s] if p == 3 else where, dst_ref=where,
+                                            send_sem=ag_send.at[c, s, p], recv_sem=ag_recv.at[c, s, p],
+                                            device_id=peer[dim], device_id_type=MESH)
+
+    def core_copy(c, s):
+        where = dw_out.at[first + c, rows(s * block, block)]
+        return pltpu.make_async_remote_copy(src_ref=where, dst_ref=where, send_sem=c_send.at[c, s],
+                                            recv_sem=c_recv.at[c, s], device_id=peer["c"], device_id_type=MESH)
+
+    db_dims = ("x", "y", "z1", "z2")
+
+    def db_copy(p):
+        return pltpu.make_async_remote_copy(src_ref=dba.at[p], dst_ref=dbl.at[p], send_sem=db_send.at[p],
+                                            recv_sem=db_recv.at[p], device_id=peer[db_dims[p]], device_id_type=MESH)
+
+    def db_core_copy():
+        return pltpu.make_async_remote_copy(src_ref=dba.at[4], dst_ref=db_out.at[core], send_sem=db_send.at[4],
+                                            recv_sem=db_recv.at[4], device_id=peer["c"], device_id_type=MESH)
+
+    dba[0] = db_in[...]
+    db_copy(0).start()
+    for s in range(BLOCKS):
+        for c in range(layers):
+            reduce_copy(c, s, 0).start()
+    for s in range(BLOCKS):
+        for c in range(layers):
+            local_load(c, s).start()
+
+    def add(dst, src_of, size):
+        step = 8 if size >= 8 else size
+
+        def body(i, carry):
+            r = pl.ds(pl.multiple_of(i * step, step), step)
+            dst[r, :] = dst[r, :] + src_of(i * step, step)
+            return carry
+
+        lax.fori_loop(0, size // step, body, 0)
+
+    order = event_order(layers)
+    spread = max(1, len(order) // 8)
+    for n, (c, s, step) in enumerate(order):
+        if step < 4:
+            size = block >> (step + 1)
+            reduce_copy(c, s, step).wait_recv()
+            if step == 0:
+                local_load(c, s).wait()
+                add(land0.at[c, s], lambda i, k: loc[c, s, rows(i, k), :], size)
+            else:
+                keep = bits[ORDERS[c][s][step]] * size
+                add(land[step].at[c, s], lambda i, k: land[step - 1][c, s, rows(keep + i, k), :], size)
+            if step < 3:
+                reduce_copy(c, s, step + 1).start()
+            else:
+                put(c, s).start()
+                gather_copy(c, s, 3).start()
+        else:
+            p = 7 - step
+            if p == 3:
+                put(c, s).wait()
+            gather_copy(c, s, p).wait_recv()
+            if p > 0:
+                gather_copy(c, s, p - 1).start()
+            else:
+                core_copy(c, s).start()
+        if n % spread == spread - 1 and n // spread < 4:
+            p = n // spread
+            db_copy(p).wait_recv()
+            dba[p + 1] = dba[p] + dbl[p]
+            if p < 3:
+                db_copy(p + 1).start()
+            else:
+                db_core_copy().start()
+                db_out[core] = dba[4]
+
+    for s in range(BLOCKS):
+        for c in range(layers):
+            core_copy(c, s).wait_recv()
+            core_copy(c, s).wait_send()
+            for p in range(4):
+                reduce_copy(c, s, p).wait_send()
+                gather_copy(c, s, p).wait_send()
+    db_core_copy().wait()
+    for p in range(4):
+        db_copy(p).wait_send()
+
+
+def sum_over_chips(dw, db):
+    layers, n_rows, n_cols = dw.shape
+    block = n_rows // BLOCKS
+    f32 = jnp.float32
+    vmem = pl.BlockSpec(memory_space=pltpu.VMEM)
+    hbm = pl.BlockSpec(memory_space=pl.ANY)
+    dma = pltpu.SemaphoreType.DMA
+    return pl.pallas_call(
+        functools.partial(sum_kernel, layers),
+        out_shape=(jax.ShapeDtypeStruct((2 * layers, n_rows, n_cols), f32), jax.ShapeDtypeStruct((2,) + db.shape, f32)),
+        in_specs=[hbm, vmem],
+        out_specs=(hbm, vmem),
+        scratch_shapes=[
+            pltpu.VMEM((layers, BLOCKS, block // 2, n_cols), f32), pltpu.VMEM((layers, BLOCKS, block // 2, n_cols), f32),
+            pltpu.VMEM((layers, BLOCKS, block // 4, n_cols), f32), pltpu.VMEM((layers, BLOCKS, block // 8, n_cols), f32),
+            pltpu.VMEM((layers, BLOCKS, block // 16, n_cols), f32),
+            pltpu.VMEM((4,) + db.shape, f32), pltpu.VMEM((5,) + db.shape, f32),
+            dma((layers, BLOCKS)), dma((layers, BLOCKS)), dma((layers, BLOCKS, 4)), dma((layers, BLOCKS, 4)),
+            dma((layers, BLOCKS, 4)), dma((layers, BLOCKS, 4)), dma((layers, BLOCKS)), dma((layers, BLOCKS)),
+            dma((5,)), dma((5,)),
+        ],
+        compiler_params=pltpu.CompilerParams(collective_id=1, has_side_effects=True, vmem_limit_bytes=66_000_000),
+        name="sum",
+    )(dw, db)
+
+
 def solution(mesh):
     batch_axes = tuple(mesh.axis_names)
 
     def device_step(x_in, d_out, weights, biases):
+        layers = weights.shape[0] // 2
         dw, db, dx = run_stack(jnp.swapaxes(x_in, 0, 1), jnp.swapaxes(d_out, 0, 1), weights, biases)
-        top = lax.rem(lax.axis_index("data"), 2) == 1
-        dw_all = jnp.concatenate([jnp.where(top, 0.0, dw), jnp.where(top, dw, 0.0)])
-        db_all = jnp.concatenate([jnp.where(top, 0.0, db), jnp.where(top, db, 0.0)])
-        return lax.psum(dw_all, batch_axes), lax.psum(db_all, batch_axes), jnp.swapaxes(dx, 0, 1)
+        dw_all, db_all = sum_over_chips(dw, db)
+        return dw_all, db_all[:, :layers].reshape(biases.shape), jnp.swapaxes(dx, 0, 1)
 
     return jax.shard_map(device_step, mesh=mesh,
                          in_specs=(P(batch_axes), P(batch_axes), P(), P()),

time: 976 us -> 592 us (0.61)
  waiting for transfers between devices: 679 us -> 0 us
  Pallas kernels: 137 us -> 549 us
  other arithmetic: 60.3 us -> 0 us
  blocking collectives: 43.9 us -> 0 us
  between operations: 14.1 us -> 0.65 us
    psum x1 -> x0, waiting for transfers between devices: 679 us -> none  [device_step(): lax.psum(dw_all, batch_axes)]
    pallas_call x0 -> x1, Pallas kernels: none -> 412 us  [sum_over_chips(): pl.pallas_call(functools.partial(sum_kernel, layers), out_shape=(jax.Shap...]
    psum x1 -> x0, blocking collectives: 43.9 us -> none  [device_step(): lax.psum(db_all, batch_axes)]
    concatenate x2 -> x0, other arithmetic: 34.5 us -> none  [the longest x1 34.5 us: device_step(): dw_all = jnp.concatenate([jnp.where(top, 0.0, dw), jnp.where(top, dw, 0.0)])]
    select_n x2 -> x0, other arithmetic: 25.8 us -> none  [the longest x1 25.7 us: device_step(): dw_all = jnp.concatenate([jnp.where(top, 0.0, dw), jnp.where(top, dw, 0.0)])]
    unnamed x8 -> x4, local copies, waits for them, and re-layouts: 40.6 us -> 40.6 us
  transfers between devices with their start and end apart: 1 -> 0, of which waited for: 1 -> 0; matrix products, arithmetic and copies ran while one was open for 0% -> 0% of each run, Pallas kernels for 0% -> 0%
where the time goes in v1:
time: 592 us
  Pallas kernels  549 us (93%)
  local copies, waits for them, and re-layouts  42.2 us (7%)
    pallas_call x1, Pallas kernels, sum_over_chips(): pl.pallas_call(functools.partial(sum_kernel, layers), out_shape=(jax.Shap...  412 us
    pallas_call x1, Pallas kernels, run_stack(): pl.pallas_call(functools.partial(stack_kernel, steps, half, layers), out_...  137 us
    unnamed x4, local copies, waits for them, and re-layouts  40.6 us

profile of v1, /device:TPU:0, one launch (start us, length us, event | category | flops | bytes accessed | tf_op | source)
XLA Modules:
  0.0 591.8 jit_solution(17138997961061829634)
XLA Ops:
  0.6 1.8 copy.16
  2.4 2.1 copy.15
  4.6 137.3 %stack.1 = (f32[3,1024,2048]{2,1,0:T(8,128)}, f32[8,2048]{1,0:T(8,128)}, f32[32,8,512]{2,1,0:T(8,128)}) custom-call(bf16[32,8,512]{2,1,0:T(8,128)(2,1)} %bitcast.8, f32[32,8,512]{2,1,0:T(8,128)} %bitcast.7, bf16[6,1024,2048]{2,1,0:T(8,128)(2,1)} %w_hbm.1, f32[6,2048]{1,0:T(8,128)} %b_ref.1), custom_call_target="tpu_custom_call" | custom-call | tf_op jit(solution)/shard_map/stack/pallas_call | solution.py:300
  141.8 2.1 copy.12
  144.0 411.7 %sum.1 = (f32[6,1024,2048]{2,1,0:T(8,128)}, f32[2,8,2048]{2,1,0:T(8,128)}) custom-call(f32[3,1024,2048]{2,1,0:T(8,128)} %get-tuple-element.8.dw_in, f32[8,2048]{1,0:T(8,128)} %get-tuple-element.9.db_in), custom_call_target="tpu_custom_call" | custom-call | tf_op jit(solution)/shard_map/sum/pallas_call | solution.py:496
  555.7 0.9 slice.3
  556.6 0.7 reshape.9
  557.3 34.5 %copy.18 = f32[6,1024,2048]{2,1,0:T(8,128)} copy(f32[6,1024,2048]{2,1,0:T(8,128)} %get-tuple-element.22) | data formatting | bytes 100663296

commit v2 on v1

--- a/solution.py
+++ b/solution.py
@@ -18,34 +18,49 @@
     return 0.5 * jnp.tanh(0.5 * z) + 0.5
 
 
+PAIR = ("x", "y", "z1")
+
+
+def chip_map():
+    z = lax.axis_index("rep")
+    d = lax.axis_index("data")
+    core = lax.rem(d, 2)
+    bits = {"x": lax.rem(d // 2, 2), "y": d // 4, "z1": lax.rem(z, 2), "z2": z // 2}
+    peers = {"x": (z, d + 2 - 4 * bits["x"]), "y": (z, d + 4 - 8 * bits["y"]), "z1": (z + 1 - 2 * bits["z1"], d),
+             "z2": (z + 2 - 4 * bits["z2"], d), "c": (z, d + 1 - 2 * core)}
+    return bits, peers, core
+
+
 def stack_kernel(steps, half, layers, x_ref, dy_ref, w_hbm, b_ref, dw_hbm, db_ref, dx_ref,
-                 w, wt, xs, hs, gates, cs, xp, dzs, dys, xb, dyb, dxs, dr_s, dc_s, dbacc, xt, stage,
-                 w_sem, in_send, in_recv, fsend, frecv, bsend, brecv, dx_send, dx_recv, out_sem):
+                 w, wt, xs, hs, gates, cs, xp, dzs, dys, xb, dyb, dr_s, dc_s, dbacc, xt, stage, xs_p, hs_p, dzs_p,
+                 w_sem, in_send, in_recv, fsend, frecv, bsend, brecv, dx_send, dx_recv, out_sem,
+                 a_send, a_recv, z_send, z_recv):
     rows = 2 * half
     chunk = T * rows
     n_chunks = steps // T
-    me = lax.axis_index("data")
-    core = lax.rem(me, 2)
-    partner = me + 1 - 2 * core
+    bits, peers, core = chip_map()
+    partner = peers["c"]
     first = core * layers
 
     barrier = pltpu.get_barrier_semaphore()
-    pl.semaphore_signal(barrier, inc=1, device_id={"data": partner}, device_id_type=MESH)
+    greet = [partner] + [peers[dim] for dim in PAIR]
+    for p in greet:
+        pl.semaphore_signal(barrier, inc=1, device_id=p, device_id_type=MESH)
 
     def weight_copy(l):
         return pltpu.make_async_copy(w_hbm.at[first + l], w.at[l], w_sem.at[l])
 
     for l in range(layers):
         weight_copy(l).start()
-    pl.semaphore_wait(barrier, 1)
+    pl.semaphore_wait(barrier, len(greet))
 
     def x_copy():
         return pltpu.make_async_remote_copy(src_ref=x_ref, dst_ref=xb, send_sem=in_send.at[0], recv_sem=in_recv.at[0],
-                                            device_id={"data": partner}, device_id_type=MESH)
+                                            device_id=partner, device_id_type=MESH)
 
     def dy_copy():
         return pltpu.make_async_remote_copy(src_ref=dy_ref, dst_ref=dyb, send_sem=in_send.at[1], recv_sem=in_recv.at[1],
-                                            device_id={"data": partner}, device_id_type=MESH)
+                                            device_id=partner, device_id_type=MESH)
 
     def chunk_rows(k):
         return pl.ds(pl.multiple_of(k * chunk, chunk), chunk)
@@ -53,16 +68,28 @@
     def f_copy(k):
         return pltpu.make_async_remote_copy(src_ref=xs.at[layers, chunk_rows(k)], dst_ref=xs.at[0, chunk_rows(k)],
                                             send_sem=fsend.at[k], recv_sem=frecv.at[k],
-                                            device_id={"data": partner}, device_id_type=MESH)
+                                            device_id=partner, device_id_type=MESH)
 
     def b_copy(k):
         return pltpu.make_async_remote_copy(src_ref=dys.at[1, chunk_rows(k)], dst_ref=dys.at[0, chunk_rows(k)],
                                             send_sem=bsend.at[k], recv_sem=brecv.at[k],
-                                            device_id={"data": partner}, device_id_type=MESH)
+                                            device_id=partner, device_id_type=MESH)
 
     def dx_copy():
-        return pltpu.make_async_remote_copy(src_ref=dxs, dst_ref=dx_ref, send_sem=dx_send, recv_sem=dx_recv,
-                                            device_id={"data": partner}, device_id_type=MESH)
+        return pltpu.make_async_remote_copy(src_ref=dyb, dst_ref=dx_ref, send_sem=dx_send, recv_sem=dx_recv,
+                                            device_id=partner, device_id_type=MESH)
+
+    def act_copy(l, part):
+        src, dst = ((xs, xs_p), (hs, hs_p))[part]
+        return pltpu.make_async_remote_copy(src_ref=src.at[l, pl.ds(0, steps * rows)], dst_ref=dst.at[l],
+                                            send_sem=a_send.at[l, part], recv_sem=a_recv.at[l, part],
+                                            device_id=peers[PAIR[l]], device_id_type=MESH)
+
+    def dz_copy(l, k):
+        cols = pl.ds(pl.multiple_of((1 - bits[PAIR[l]]) * (G // 2), G // 2), G // 2)
+        return pltpu.make_async_remote_copy(src_ref=dzs.at[l, chunk_rows(k), cols], dst_ref=dzs_p.at[l, chunk_rows(k)],
+                                            send_sem=z_send.at[l, k], recv_sem=z_recv.at[l, k],
+                                            device_id=peers[PAIR[l]], device_id_type=MESH)
 
     @pl.when(core == 1)
     def _():
@@ -143,6 +170,10 @@
         return carry
 
     lax.fori_loop(0, n_chunks, fwd_chunk, 0)
+
+    for l in range(layers):
+        for part in range(2):
+            act_copy(l, part).start()
 
     def transpose_weights(i, carry):
         l = i // 8
@@ -209,6 +240,9 @@
         def _():
             b_copy(k).start()
 
+        for l in range(layers):
+            dz_copy(l, k).start()
+
         return carry
 
     lax.fori_loop(0, n_chunks, bwd_chunk, 0)
@@ -218,7 +252,7 @@
         def split(t, carry):
             both = dys[1, pl.ds(pl.multiple_of(t * rows, rows), rows), :]
             dx_ref[t] = both[:half]
-            dxs[t] = both[half:]
+            dyb[t] = both[half:]
             return carry
 
         lax.fori_loop(0, steps, split, 0)
@@ -230,39 +264,44 @@
 
     n_rows = steps * rows
 
-    def out_copy(i):
-        l = i // 4
-        b = lax.rem(i, 4)
-        return pltpu.make_async_copy(stage.at[lax.rem(i, 2)], dw_hbm.at[l, pl.ds(pl.multiple_of(b * 256, 256), 256)],
-                                     out_sem.at[lax.rem(i, 2)])
-
-    def dw_block(i, carry):
-        l = i // 4
-        b = lax.rem(i, 4)
-
-        @pl.when(i >= 2)
-        def _():
-            out_copy(i - 2).wait()
-
-        cols = pl.ds(pl.multiple_of(lax.rem(b, 2) * 256, 256), 256)
-
-        @pl.when(b < 2)
-        def _():
-            xt[...] = xs[l, :, cols].T
-
-        @pl.when(b >= 2)
-        def _():
-            xt[...] = hs[l, :n_rows, cols].T
-
-        for q in range(4):
-            stage[lax.rem(i, 2), :, q * H:(q + 1) * H] = jnp.dot(xt[...], dzs[l, :, q * H:(q + 1) * H],
-                                                                preferred_element_type=jnp.float32)
-        out_copy(i).start()
-        return carry
-
-    lax.fori_loop(0, layers * 4, dw_block, 0)
-    out_copy(layers * 4 - 2).wait()
-    out_copy(layers * 4 - 1).wait()
+    n_out = 2 * H // 256
+
+    def out_copy(l, b):
+        slot = b % 2
+        return pltpu.make_async_copy(stage.at[slot], dw_hbm.at[l, pl.ds(b * 256, 256)], out_sem.at[slot])
+
+    for l in range(layers):
+        own = pl.ds(pl.multiple_of(bits[PAIR[l]] * (G // 2), G // 2), G // 2)
+        for part in range(2):
+            act_copy(l, part).wait_recv()
+
+        def arrived(k, carry):
+            dz_copy(l, k).wait_recv()
+            return carry
+
+        lax.fori_loop(0, n_chunks, arrived, 0)
+        for b in range(n_out):
+            mine, theirs = ((xs, xs_p), (hs, hs_p))[b * 256 // H]
+            cols = slice(b * 256 % H, b * 256 % H + 256)
+            if l * n_out + b >= 2:
+                out_copy(l if b >= 2 else l - 1, (b - 2) % n_out).wait()
+            xt[:, :n_rows] = mine[l, :n_rows, cols].T
+            xt[:, n_rows:] = theirs[l, :, cols].T
+            stage[b % 2] = (jnp.dot(xt[:, :n_rows], dzs[l, :, own], preferred_element_type=jnp.float32)
+                            + jnp.dot(xt[:, n_rows:], dzs_p[l], preferred_element_type=jnp.float32))
+            out_copy(l, b).start()
+    out_copy(layers - 1, n_out - 2).wait()
+    out_copy(layers - 1, n_out - 1).wait()
+
+    for l in range(layers):
+        for part in range(2):
+            act_copy(l, part).wait_send()
+
+        def sent(k, carry):
+            dz_copy(l, k).wait_send()
+            return carry
+
+        lax.fori_loop(0, n_chunks, sent, 0)
 
     @pl.when(core == 0)
     def _():
@@ -299,7 +338,7 @@
     dma = pltpu.SemaphoreType.DMA
     return pl.pallas_call(
         functools.partial(stack_kernel, steps, half, layers),
-        out_shape=(jax.ShapeDtypeStruct((layers, 2 * H, G), f32), jax.ShapeDtypeStruct((8, G), f32),
+        out_shape=(jax.ShapeDtypeStruct((layers, 2 * H, G // 2), f32), jax.ShapeDtypeStruct((8, G), f32),
                    jax.ShapeDtypeStruct((steps, half, H), f32)),
         in_specs=[vmem, vmem, hbm, vmem],
         out_specs=(hbm, vmem, vmem),
@@ -309,62 +348,56 @@
             pltpu.VMEM((layers, n, G), f32), pltpu.VMEM((layers, n + rows, H), f32),
             pltpu.VMEM((T * rows, G), f32), pltpu.VMEM((layers, n, G), bf),
             pltpu.VMEM((2, n, H), f32), pltpu.VMEM((steps, half, H), bf),
-            pltpu.VMEM((steps, half, H), f32), pltpu.VMEM((steps, half, H), f32),
+            pltpu.VMEM((steps, half, H), f32),
             pltpu.VMEM((layers, rows, H), f32), pltpu.VMEM((layers, rows, H), f32),
-            pltpu.VMEM((layers, rows, G), f32), pltpu.VMEM((256, n), bf), pltpu.VMEM((2, 256, G), f32),
+            pltpu.VMEM((layers, rows, G), f32), pltpu.VMEM((256, 2 * n), bf), pltpu.VMEM((2, 256, G // 2), f32),
+            pltpu.VMEM((layers, n, H), bf), pltpu.VMEM((layers, n, H), bf), pltpu.VMEM((layers, n, G // 2), bf),
             dma((layers,)), dma((2,)), dma((2,)), dma((n_chunks,)), dma((n_chunks,)), dma((n_chunks,)), dma((n_chunks,)),
             dma, dma, dma((2,)),
+            dma((layers, 2)), dma((layers, 2)), dma((layers, n_chunks)), dma((layers, n_chunks)),
         ],
-        compiler_params=pltpu.CompilerParams(collective_id=0, has_side_effects=True, vmem_limit_bytes=66_000_000),
+        compiler_params=pltpu.CompilerParams(collective_id=0, has_side_effects=True, vmem_limit_bytes=67_000_000),
         name="stack",
     )(x_t, dy_t, weights, biases)
 
 
-BLOCKS = 4
-ORDERS = ((("x", "y", "z1", "z2"),) * BLOCKS,
-          (("y", "x", "z1", "z2"),) * BLOCKS,
-          (("z1", "x", "y", "z2"), ("z1", "y", "x", "z2")) * (BLOCKS // 2))
+BLOCKS = 8
+ORDERS = ((("y", "z1", "z2"),) * BLOCKS,
+          (("x", "z1", "z2"),) * BLOCKS,
+          (("x", "y", "z2"), ("y", "x", "z2")) * (BLOCKS // 2))
 
 
 def event_order(layers):
     free = {"x": 0.0, "y": 0.0, "z": 0.0}
     pending = []
 
-    def send(now, c, s, step, dim, size):
+    def send(now, c, s, step):
+        q = step if step < 3 else 5 - step
+        dim = PAIR[c] if step == 6 else ORDERS[c][s][q]
         link = dim[0]
-        start = max(now, free[link])
-        free[link] = start + size * (1.5 if dim == "z2" else 1.0)
+        free[link] = max(now, free[link]) + 0.5 ** q * (1.5 if dim == "z2" else 1.0)
         pending.append((free[link] + 0.1, s, c, step))
 
     for s in range(BLOCKS):
         for c in range(layers):
-            send(0.0, c, s, 0, ORDERS[c][s][0], 1.0)
+            send(0.0, c, s, 0)
     order = []
     while pending:
         pending.sort()
         now, s, c, step = pending.pop(0)
         order.append((c, s, step))
-        if step < 7:
-            p = step + 1 if step < 3 else 6 - step
-            send(now, c, s, step + 1, ORDERS[c][s][p], 0.5 ** p)
+        if step < 6:
+            send(now, c, s, step + 1)
     return order
 
 
-def sum_kernel(layers, dw_in, db_in, dw_out, db_out, loc, land0, land1, land2, land3, dbl, dba,
+def sum_kernel(layers, dw_in, db_in, dw_out, db_out, loc, land0, land1, land2, dbl, dba,
                loc_sem, put_sem, rs_send, rs_recv, ag_send, ag_recv, c_send, c_recv, db_send, db_recv):
-    land = (land0, land1, land2, land3)
-    z = lax.axis_index("rep")
-    d = lax.axis_index("data")
-    core = lax.rem(d, 2)
-    x_bit = lax.rem(d // 2, 2)
-    y_bit = d // 4
-    z1_bit = lax.rem(z, 2)
-    z2_bit = z // 2
-    bits = {"x": x_bit, "y": y_bit, "z1": z1_bit, "z2": z2_bit}
-    peer = {"x": (z, d + 2 - 4 * x_bit), "y": (z, d + 4 - 8 * y_bit), "z1": (z + 1 - 2 * z1_bit, d),
-            "z2": (z + 2 - 4 * z2_bit, d), "c": (z, d + 1 - 2 * core)}
+    land = (land0, land1, land2)
+    bits, peer, core = chip_map()
     first = core * layers
     block = dw_in.shape[1] // BLOCKS
+    width = dw_in.shape[2]
 
     barrier = pltpu.get_barrier_semaphore()
     for p in peer.values():
@@ -374,34 +407,38 @@
     def rows(off, size):
         return pl.ds(pl.multiple_of(off, 8), size)
 
+    def own_cols(c):
+        return pl.ds(pl.multiple_of(bits[PAIR[c]] * width, width), width)
+
     def offset(c, s, steps):
         off = s * block
-        for p in range(steps):
-            off = off + bits[ORDERS[c][s][p]] * (block >> (p + 1))
+        for q in range(steps):
+            off = off + bits[ORDERS[c][s][q]] * (block >> (q + 1))
         return off
 
     def local_load(c, s):
         return pltpu.make_async_copy(dw_in.at[c, rows(offset(c, s, 1), block // 2)], loc.at[c, s], loc_sem.at[c, s])
 
-    def reduce_copy(c, s, p):
-        dim = ORDERS[c][s][p]
-        size = block >> (p + 1)
-        if p == 0:
+    def reduce_copy(c, s, q):
+        dim = ORDERS[c][s][q]
+        size = block >> (q + 1)
+        if q == 0:
             src = dw_in.at[c, rows(s * block + (1 - bits[dim]) * size, size)]
         else:
-            src = land[p - 1].at[c, s, rows((1 - bits[dim]) * size, size)]
-        return pltpu.make_async_remote_copy(src_ref=src, dst_ref=land[p].at[c, s], send_sem=rs_send.at[c, s, p],
-                                            recv_sem=rs_recv.at[c, s, p], device_id=peer[dim], device_id_type=MESH)
+            src = land[q - 1].at[c, s, rows((1 - bits[dim]) * size, size)]
+        return pltpu.make_async_remote_copy(src_ref=src, dst_ref=land[q].at[c, s], send_sem=rs_send.at[c, s, q],
+                                            recv_sem=rs_recv.at[c, s, q], device_id=peer[dim], device_id_type=MESH)
 
     def put(c, s):
-        return pltpu.make_async_copy(land3.at[c, s], dw_out.at[first + c, rows(offset(c, s, 4), block // 16)],
+        return pltpu.make_async_copy(land2.at[c, s], dw_out.at[first + c, rows(offset(c, s, 3), block // 8), own_cols(c)],
                                      put_sem.at[c, s])
 
-    def gather_copy(c, s, p):
-        dim = ORDERS[c][s][p]
-        where = dw_out.at[first + c, rows(offset(c, s, p + 1), block >> (p + 1))]
-        return pltpu.make_async_remote_copy(src_ref=land3.at[c, s] if p == 3 else where, dst_ref=where,
-                                            send_sem=ag_send.at[c, s, p], recv_sem=ag_recv.at[c, s, p],
+    def gather_copy(c, s, step):
+        q = 5 - step
+        dim = PAIR[c] if q < 0 else ORDERS[c][s][q]
+        where = dw_out.at[first + c, rows(offset(c, s, q + 1), block >> (q + 1)), own_cols(c)]
+        return pltpu.make_async_remote_copy(src_ref=land2.at[c, s] if q == 2 else where, dst_ref=where,
+                                            send_sem=ag_send.at[c, s, step - 3], recv_sem=ag_recv.at[c, s, step - 3],
                                             device_id=peer[dim], device_id_type=MESH)
 
     def core_copy(c, s):
@@ -429,39 +466,36 @@
             local_load(c, s).start()
 
     def add(dst, src_of, size):
-        step = 8 if size >= 8 else size
-
         def body(i, carry):
-            r = pl.ds(pl.multiple_of(i * step, step), step)
-            dst[r, :] = dst[r, :] + src_of(i * step, step)
-            return carry
-
-        lax.fori_loop(0, size // step, body, 0)
+            r = pl.ds(pl.multiple_of(i * 8, 8), 8)
+            dst[r, :] = dst[r, :] + src_of(i * 8)
+            return carry
+
+        lax.fori_loop(0, size // 8, body, 0)
 
     order = event_order(layers)
     spread = max(1, len(order) // 8)
     for n, (c, s, step) in enumerate(order):
-        if step < 4:
+        if step < 3:
             size = block >> (step + 1)
             reduce_copy(c, s, step).wait_recv()
             if step == 0:
                 local_load(c, s).wait()
-                add(land0.at[c, s], lambda i, k: loc[c, s, rows(i, k), :], size)
+                add(land0.at[c, s], lambda i: loc[c, s, rows(i, 8), :], size)
             else:
                 keep = bits[ORDERS[c][s][step]] * size
-                add(land[step].at[c, s], lambda i, k: land[step - 1][c, s, rows(keep + i, k), :], size)
-            if step < 3:
+                add(land[step].at[c, s], lambda i: land[step - 1][c, s, rows(keep + i, 8), :], size)
+            if step < 2:
                 reduce_copy(c, s, step + 1).start()
             else:
                 put(c, s).start()
                 gather_copy(c, s, 3).start()
         else:
-            p = 7 - step
-            if p == 3:
+            if step == 3:
                 put(c, s).wait()
-            gather_copy(c, s, p).wait_recv()
-            if p > 0:
-                gather_copy(c, s, p - 1).start()
+            gather_copy(c, s, step).wait_recv()
+            if step < 6:
+                gather_copy(c, s, step + 1).start()
             else:
                 core_copy(c, s).start()
         if n % spread == spread - 1 and n // spread < 4:
@@ -478,9 +512,10 @@
         for c in range(layers):
             core_copy(c, s).wait_recv()
             core_copy(c, s).wait_send()
-            for p in range(4):
-                reduce_copy(c, s, p).wait_send()
-                gather_copy(c, s, p).wait_send()
+            for q in range(3):
+                reduce_copy(c, s, q).wait_send()
+            for step in range(3, 7):
+                gather_copy(c, s, step).wait_send()
     db_core_copy().wait()
     for p in range(4):
         db_copy(p).wait_send()
@@ -495,19 +530,18 @@
     dma = pltpu.SemaphoreType.DMA
     return pl.pallas_call(
         functools.partial(sum_kernel, layers),
-        out_shape=(jax.ShapeDtypeStruct((2 * layers, n_rows, n_cols), f32), jax.ShapeDtypeStruct((2,) + db.shape, f32)),
+        out_shape=(jax.ShapeDtypeStruct((2 * layers, n_rows, 2 * n_cols), f32), jax.ShapeDtypeStruct((2,) + db.shape, f32)),
         in_specs=[hbm, vmem],
         out_specs=(hbm, vmem),
         scratch_shapes=[
             pltpu.VMEM((layers, BLOCKS, block // 2, n_cols), f32), pltpu.VMEM((layers, BLOCKS, block // 2, n_cols), f32),
             pltpu.VMEM((layers, BLOCKS, block // 4, n_cols), f32), pltpu.VMEM((layers, BLOCKS, block // 8, n_cols), f32),
-            pltpu.VMEM((layers, BLOCKS, block // 16, n_cols), f32),
             pltpu.VMEM((4,) + db.shape, f32), pltpu.VMEM((5,) + db.shape, f32),
-            dma((layers, BLOCKS)), dma((layers, BLOCKS)), dma((layers, BLOCKS, 4)), dma((layers, BLOCKS, 4)),
+            dma((layers, BLOCKS)), dma((layers, BLOCKS)), dma((layers, BLOCKS, 3)), dma((layers, BLOCKS, 3)),
             dma((layers, BLOCKS, 4)), dma((layers, BLOCKS, 4)), dma((layers, BLOCKS)), dma((layers, BLOCKS)),
             dma((5,)), dma((5,)),
         ],
-        compiler_params=pltpu.CompilerParams(collective_id=1, has_side_effects=True, vmem_limit_bytes=66_000_000),
+        compiler_params=pltpu.CompilerParams(collective_id=1, has_side_effects=True, vmem_limit_bytes=67_000_000),
         name="sum",
     )(dw, db)
 

time: 592 us -> 475 us (0.80)
  Pallas kernels: 549 us -> 432 us
    pallas_call x1, Pallas kernels: 412 us -> 290 us  [sum_over_chips(): pl.pallas_call(functools.partial(sum_kernel, layers), out_shape=(jax.Shap...]
where the time goes in v2:
time: 475 us
  Pallas kernels  432 us (91%)
  local copies, waits for them, and re-layouts  42.2 us (9%)
    pallas_call x1, Pallas kernels, sum_over_chips(): pl.pallas_call(functools.partial(sum_kernel, layers), out_shape=(jax.Shap...  290 us
    pallas_call x1, Pallas kernels, run_stack(): pl.pallas_call(functools.partial(stack_kernel, steps, half, layers), out_...  141 us
    unnamed x4, local copies, waits for them, and re-layouts  40.6 us

profile of v2, /device:TPU:0, one launch (start us, length us, event | category | flops | bytes accessed | tf_op | source)
XLA Modules:
  0.0 474.6 jit_solution(14064990813802311341)
XLA Ops:
  0.6 1.8 copy.16
  2.4 2.1 copy.15
  4.6 141.3 %stack.1 = (f32[3,1024,1024]{2,1,0:T(8,128)}, f32[8,2048]{1,0:T(8,128)}, f32[32,8,512]{2,1,0:T(8,128)}) custom-call(bf16[32,8,512]{2,1,0:T(8,128)(2,1)} %bitcast.8, f32[32,8,512]{2,1,0:T(8,128)} %bitcast.7, bf16[6,1024,2048]{2,1,0:T(8,128)(2,1)} %w_hbm.1, f32[6,2048]{1,0:T(8,128)} %b_ref.1), custom_call_target="tpu_custom_call" | custom-call | tf_op jit(solution)/shard_map/stack/pallas_call | solution.py:339
  145.9 2.1 copy.12
  148.0 290.4 %sum.1 = (f32[6,1024,2048]{2,1,0:T(8,128)}, f32[2,8,2048]{2,1,0:T(8,128)}) custom-call(f32[3,1024,1024]{2,1,0:T(8,128)} %get-tuple-element.8.dw_in, f32[8,2048]{1,0:T(8,128)} %get-tuple-element.9.db_in), custom_call_target="tpu_custom_call" | custom-call | tf_op jit(solution)/shard_map/sum/pallas_call | solution.py:531
  438.5 0.9 slice.3
  439.4 0.7 reshape.9
  440.1 34.5 %copy.18 = f32[6,1024,2048]{2,1,0:T(8,128)} copy(f32[6,1024,2048]{2,1,0:T(8,128)} %get-tuple-element.22) | data formatting | bytes 100663296

commit v3 on v2

--- a/solution.py
+++ b/solution.py
@@ -10,7 +10,7 @@
 MESH = pl.DeviceIdType.MESH
 H = 512
 G = 4 * H
-T = 4
+T = 8
 HB = 256
 
 
@@ -117,8 +117,31 @@
 
         lax.fori_loop(0, steps, join, 0)
 
+    def transpose_weights(i, carry):
+        l = i // 8
+        j = lax.rem(i, 8)
+        cols = pl.ds(pl.multiple_of(j * 256, 256), 256)
+        wt[l, cols, :] = w[l, :, cols].T
+        return carry
+
+    @pl.when(core == 1)
+    def _():
+        for l in range(layers):
+            weight_copy(l).wait()
+        lax.fori_loop(0, layers * 8, transpose_weights, 0)
+
+    @pl.when(core == 1)
+    def _():
+        dy_copy().wait_recv()
+
+        def join(t, carry):
+            dys[0, pl.ds(pl.multiple_of(t * rows, rows), rows), :] = jnp.concatenate([dyb[t], dy_ref[t]], axis=0)
+            return carry
+
+        lax.fori_loop(0, steps, join, 0)
+
     def fwd_layer(k, l):
-        @pl.when(k == 0)
+        @pl.when((k == 0) & (core == 0))
         def _():
             weight_copy(l).wait()
 
@@ -175,24 +198,9 @@
         for part in range(2):
             act_copy(l, part).start()
 
-    def transpose_weights(i, carry):
-        l = i // 8
-        j = lax.rem(i, 8)
-        cols = pl.ds(pl.multiple_of(j * 256, 256), 256)
-        wt[l, cols, :] = w[l, :, cols].T
-        return carry
-
-    lax.fori_loop(0, layers * 8, transpose_weights, 0)
-
-    @pl.when(core == 1)
-    def _():
-        dy_copy().wait_recv()
-
-        def join(t, carry):
-            dys[0, pl.ds(pl.multiple_of(t * rows, rows), rows), :] = jnp.concatenate([dyb[t], dy_ref[t]], axis=0)
-            return carry
-
-        lax.fori_loop(0, steps, join, 0)
+    @pl.when(core == 0)
+    def _():
+        lax.fori_loop(0, layers * 8, transpose_weights, 0)
 
     def bwd_layer(k, l, src):
         def step(i, carry):
@@ -362,6 +370,8 @@
 
 
 BLOCKS = 8
+DEPTH = 4
+TRIGGER = 2
 ORDERS = ((("y", "z1", "z2"),) * BLOCKS,
           (("x", "z1", "z2"),) * BLOCKS,
           (("x", "y", "z2"), ("y", "x", "z2")) * (BLOCKS // 2))
@@ -375,10 +385,10 @@
         q = step if step < 3 else 5 - step
         dim = PAIR[c] if step == 6 else ORDERS[c][s][q]
         link = dim[0]
-        free[link] = max(now, free[link]) + 0.5 ** q * (1.5 if dim == "z2" else 1.0)
-        pending.append((free[link] + 0.1, s, c, step))
-
-    for s in range(BLOCKS):
+        free[link] = max(now, free[link]) + 0.5 ** q * (1.0 if dim == "z2" else 1.0)
+        pending.append((free[link] + 0.5, s, c, step))
+
+    for s in range(DEPTH):
         for c in range(layers):
             send(0.0, c, s, 0)
     order = []
@@ -388,6 +398,8 @@
         order.append((c, s, step))
         if step < 6:
             send(now, c, s, step + 1)
+        if step == TRIGGER and s + DEPTH < BLOCKS:
+            send(now, c, s + DEPTH, 0)
     return order
 
 
@@ -458,7 +470,7 @@
 
     dba[0] = db_in[...]
     db_copy(0).start()
-    for s in range(BLOCKS):
+    for s in range(DEPTH):
         for c in range(layers):
             reduce_copy(c, s, 0).start()
     for s in range(BLOCKS):
@@ -498,6 +510,8 @@
                 gather_copy(c, s, step + 1).start()
             else:
                 core_copy(c, s).start()
+        if step == TRIGGER and s + DEPTH < BLOCKS:
+            reduce_copy(c, s + DEPTH, 0).start()
         if n % spread == spread - 1 and n // spread < 4:
             p = n // spread
             db_copy(p).wait_recv()

time: 475 us -> 450 us (0.947)
  Pallas kernels: 432 us -> 406 us
    pallas_call x1, Pallas kernels: 290 us -> 271 us  [sum_over_chips(): pl.pallas_call(functools.partial(sum_kernel, layers), out_shape=(jax.Shap...]
    pallas_call x1, Pallas kernels: 141 us -> 135 us  [run_stack(): pl.pallas_call(functools.partial(stack_kernel, steps, half, layers), out_...]
where the time goes in v3:
time: 450 us; the launch traced here: 449 us
  Pallas kernels  406 us (90%)
  local copies, waits for them, and re-layouts  42.2 us (9%)
    pallas_call x1, Pallas kernels, sum_over_chips(): pl.pallas_call(functools.partial(sum_kernel, layers), out_shape=(jax.Shap...  271 us
    pallas_call x1, Pallas kernels, run_stack(): pl.pallas_call(functools.partial(stack_kernel, steps, half, layers), out_...  135 us
    unnamed x4, local copies, waits for them, and re-layouts  40.6 us

profile of v3, /device:TPU:0, one launch (start us, length us, event | category | flops | bytes accessed | tf_op | source)
XLA Modules:
  0.0 448.7 jit_solution(9050956846137604204)
XLA Ops:
  0.6 1.8 copy.16
  2.4 2.1 copy.15
  4.6 134.8 %stack.1 = (f32[3,1024,1024]{2,1,0:T(8,128)}, f32[8,2048]{1,0:T(8,128)}, f32[32,8,512]{2,1,0:T(8,128)}) custom-call(bf16[32,8,512]{2,1,0:T(8,128)(2,1)} %bitcast.8, f32[32,8,512]{2,1,0:T(8,128)} %bitcast.7, bf16[6,1024,2048]{2,1,0:T(8,128)(2,1)} %w_hbm.1, f32[6,2048]{1,0:T(8,128)} %b_ref.1), custom_call_target="tpu_custom_call" | custom-call | tf_op jit(solution)/shard_map/stack/pallas_call | solution.py:347
  139.4 2.1 copy.12
  141.5 271.1 %sum.1 = (f32[6,1024,2048]{2,1,0:T(8,128)}, f32[2,8,2048]{2,1,0:T(8,128)}) custom-call(f32[3,1024,1024]{2,1,0:T(8,128)} %get-tuple-element.8.dw_in, f32[8,2048]{1,0:T(8,128)} %get-tuple-element.9.db_in), custom_call_target="tpu_custom_call" | custom-call | tf_op jit(solution)/shard_map/sum/pallas_call | solution.py:545
  412.6 0.9 slice.3
  413.5 0.7 reshape.9
  414.2 34.5 %copy.18 = f32[6,1024,2048]{2,1,0:T(8,128)} copy(f32[6,1024,2048]{2,1,0:T(8,128)} %get-tuple-element.22) | data formatting | bytes 100663296
